TPU v7x, 32 devices: a whole 2x2x4 slice. The times are simulated.
32 devices in a mesh: heads: 4 (over y, core), tokens: 4 (over z), cols: 2 (over x).
Axes of the slice: x: 2, y: 2, z: 4, core: 2. Of those that a mesh axis runs over, the one named last changes fastest.
Arguments:
- query_in: bfloat16 [2048, 8192], P('tokens', ('heads', 'cols')), may hold values from -24 to 24
- key_in: bfloat16 [2048, 8192], P('tokens', ('heads', 'cols')), may hold values from -24 to 24
- value_in: bfloat16 [2048, 8192], P('tokens', ('heads', 'cols')), may hold values from -6 to 6
- out_grads: bfloat16 [2048, 8192], P('tokens', ('heads', 'cols')), may hold values from -6 to 6
- doc_starts: int32 [6], replicated, may hold values from 0 to 2047, as said below
Outputs:
- input_factor: float32 [8192, 8192], P('heads', ('tokens', 'cols'))
- grad_factor: float32 [8192, 8192], P('heads', ('tokens', 'cols'))
Inputs may be any that keep to these rules, and one draw needn't show every extreme that they name: Strictly increasing with the first entry 0; document d runs from doc_starts[d] to the next start (the last one to 2048) - 1. One document holds (4 // 2 + 1) * 512 tokens.
All inputs are finite; a program needn't handle non-finite values.
Results may differ from a plain program's by a relative error of at most 0.0041.
Values may be sent and summed in bfloat16 or wider, within the bound.
A program may use at most 128 MiB of HBM per device.

v0:
```python
import math

import jax
import jax.numpy as jnp
from jax import lax
from jax.sharding import PartitionSpec as P

HEAD_DIM = 128


MASK_FLOOR = -1e30


def spread(value, axis, source):
    kept = jnp.where(lax.axis_index(axis) == source, value, 0).astype(value.dtype)
    return lax.psum(kept, axis)


def document_ids(positions, doc_starts):
    return jnp.sum((positions[:, None] >= doc_starts[None, :]).astype(jnp.int32), axis=1) - 1


def pair_scores(query_rows, key_rows, query_pos, key_pos, doc_starts):
    head_count = query_rows.shape[1] // HEAD_DIM
    query_heads = query_rows.reshape(query_rows.shape[0], head_count, HEAD_DIM)
    key_heads = key_rows.reshape(key_rows.shape[0], head_count, HEAD_DIM)
    scores = jnp.einsum(
        "qhd,khd->hqk", query_heads, key_heads, preferred_element_type=jnp.float32
    ) * (1.0 / math.sqrt(HEAD_DIM))
    query_docs = document_ids(query_pos, doc_starts)
    key_docs = document_ids(key_pos, doc_starts)
    allowed = query_docs[:, None] == key_docs[None, :]
    return (scores, allowed[None, :, :])


def on_device(query_in, key_in, value_in, out_grads, doc_starts):
    tok_dev, row_width = query_in.shape
    head_count = row_width // HEAD_DIM
    first_pos = lax.axis_index("tokens") * tok_dev
    query_pos = first_pos + jnp.arange(tok_dev, dtype=jnp.int32)
    keys_all, values_all = (
        lax.all_gather(key_in, "tokens", axis=0, tiled=True),
        lax.all_gather(value_in, "tokens", axis=0, tiled=True),
    )
    all_tokens = keys_all.shape[0]
    key_span = min(512, all_tokens)
    block_ids = jnp.arange(all_tokens // key_span, dtype=jnp.int32)

    def block_scores(block_id):
        key_begin = block_id * key_span
        key_rows = lax.dynamic_slice_in_dim(keys_all, key_begin, key_span, 0)
        key_pos = key_begin + jnp.arange(key_span, dtype=jnp.int32)
        scores, allowed = pair_scores(query_in, key_rows, query_pos, key_pos, doc_starts)
        return (key_begin, scores, allowed)

    def gated(block_id, update, running):
        key_begin = block_id * key_span
        return update(running)

    def stats_step(running, block_id):

        def update(state):
            row_peak, row_mass = state
            key_begin, scores, allowed = block_scores(block_id)
            masked = jnp.where(allowed, scores, MASK_FLOOR)
            new_peak = jnp.maximum(row_peak, jnp.max(masked, axis=2))
            new_mass = row_mass * jnp.exp(row_peak - new_peak) + jnp.sum(
                jnp.where(allowed, jnp.exp(masked - new_peak[:, :, None]), 0.0), axis=2
            )
            return (new_peak, new_mass)

        return (gated(block_id, update, running), None)

    initial = (
        jnp.full((head_count, tok_dev), MASK_FLOOR, jnp.float32),
        jnp.zeros((head_count, tok_dev), jnp.float32),
    )
    (row_peak, row_mass), _ = lax.scan(stats_step, initial, block_ids)
    log_total = row_peak + jnp.log(row_mass)

    def value_step(running, block_id):

        def update(state):
            weighted, partials = state
            key_begin, scores, allowed = block_scores(block_id)
            weights = jnp.where(allowed, jnp.exp(scores - log_total[:, :, None]), 0.0).astype(
                jnp.bfloat16
            )
            value_rows = lax.dynamic_slice_in_dim(values_all, key_begin, key_span, 0).reshape(
                key_span, head_count, HEAD_DIM
            )
            weighted = weighted + jnp.einsum(
                "hqk,khd->qhd", weights, value_rows, preferred_element_type=jnp.float32
            )
            return (weighted, partials)

        return (gated(block_id, update, running), None)

    partial_rows = 8
    value_init = (
        jnp.zeros((tok_dev, head_count, HEAD_DIM), jnp.float32),
        jnp.zeros((partial_rows, row_width), jnp.float32),
    )
    (weighted, partials), _ = lax.scan(value_step, value_init, block_ids)
    attended = weighted.reshape(tok_dev, row_width).astype(jnp.bfloat16)
    stats_all = lax.all_gather(log_total.T, "tokens", axis=0, tiled=True)
    query_rows = lax.all_gather(query_in, "tokens", axis=0, tiled=True)
    grad_rows = lax.all_gather(out_grads, "tokens", axis=0, tiled=True)
    piece_rows = query_rows.shape[0]
    piece_pos = jnp.arange(piece_rows, dtype=jnp.int32)

    def update(grad_sum):
        scores, allowed = pair_scores(query_rows, key_in, piece_pos, query_pos, doc_starts)
        weights = jnp.where(allowed, jnp.exp(scores - stats_all.T[:, :, None]), 0.0).astype(
            jnp.bfloat16
        )
        piece_grads = grad_rows.reshape(piece_rows, head_count, HEAD_DIM)
        return jnp.einsum("hqk,qhd->khd", weights, piece_grads, preferred_element_type=jnp.float32)

    summed = update(jnp.zeros((tok_dev, head_count, HEAD_DIM), jnp.float32))
    value_grads = summed.reshape(tok_dev, row_width).astype(jnp.bfloat16)
    token_shards = lax.axis_size("tokens")
    col_shards = lax.axis_size("cols")
    rows_attended, rows_grads = (
        lax.all_gather(attended[None], ("tokens", "cols"), axis=0, tiled=True),
        lax.all_gather(value_grads[None], ("tokens", "cols"), axis=0, tiled=True),
    )
    rows_attended = rows_attended.reshape(token_shards, col_shards, tok_dev, row_width)
    rows_grads = rows_grads.reshape(token_shards, col_shards, tok_dev, row_width)
    own_attended = lax.dynamic_index_in_dim(
        rows_attended, lax.axis_index("cols"), 1, keepdims=False
    )
    own_grads = lax.dynamic_index_in_dim(rows_grads, lax.axis_index("cols"), 1, keepdims=False)
    cols_attended, cols_grads = (
        spread(own_attended, "heads", lax.axis_index("tokens")),
        spread(own_grads, "heads", lax.axis_index("tokens")),
    )
    input_factor = jnp.einsum(
        "acnf,ang->cfg", rows_attended, cols_attended, preferred_element_type=jnp.float32
    )
    grad_factor = jnp.einsum(
        "acnf,ang->cfg", rows_grads, cols_grads, preferred_element_type=jnp.float32
    )
    input_factor = input_factor.reshape(col_shards * row_width, row_width) / all_tokens
    grad_factor = grad_factor.reshape(col_shards * row_width, row_width) / all_tokens
    return (input_factor, grad_factor)


def solution(mesh):
    in_specs = (
        P("tokens", ("heads", "cols")),
        P("tokens", ("heads", "cols")),
        P("tokens", ("heads", "cols")),
        P("tokens", ("heads", "cols")),
        P(),
    )
    out_specs = (P("heads", ("tokens", "cols")), P("heads", ("tokens", "cols")))
    return jax.shard_map(
        on_device, mesh=mesh, in_specs=in_specs, out_specs=out_specs, check_vma=False
    )
```

profile of v0, /device:TPU:5, one launch (start us, length us, event | category | flops | bytes accessed | tf_op | source)
XLA Modules:
  0.0 773.5 jit_solution(3249628128545039161)
XLA Ops:
  7.2 2.4 copy.58
  9.7 2.3 copy.57
  12.0 0.7 all-gather.15.cloned.1.call-update
  12.8 2.3 copy.62
  15.1 76.4 %all-gather.9.cloned.1.call-done = bf16[2048,1024]{0,1:T(8,128)(2,1)} async-done(((bf16[512,1024]{0,1:T(8,128)(2,1)}), bf16[2048,1024]{0,1:T(8,128)(2,1)}) %all-gather.9.cloned.1.call-update) | async-done | bytes 4194320 | tf_op jit(solution)/shard_map/all_gather | solution.py:42
  91.6 27.0 %while.30 = (s32[]{:T(128)}, f32[8,512]{1,0:T(8,128)S(1)}, f32[8,512]{1,0:T(8,128)S(1)}, s32[6]{0:T(128)S(1)}, s32[4]{0:T(128)S(1)}, /*index=5*/bf16[2048,1024]{...) while((s32[]{:T(128)}, f32[8,512]{1,0:T(8,128)S(1)}, ...), condition=%wide.region_5.6_spmd.clone, body=%wide.region_0.5_spmd.clone.sunk | while | flops 553950208 | bytes 21995748 | solution.py:78
  91.6 0.6 dynamic_slice.60
  92.9 0.2 broadcast_compare_fusion.5
  93.2 1.3 constant_dynamic-slice_fusion.5
  94.5 1.7 fusion.59
  96.2 2.0 select_reduce_fusion.2
  98.3 0.6 dynamic_slice.60
  99.7 0.2 broadcast_compare_fusion.5
  99.9 1.4 constant_dynamic-slice_fusion.5
  101.3 1.7 fusion.59
  103.1 2.0 select_reduce_fusion.2
  105.2 0.6 dynamic_slice.60
  106.5 0.2 broadcast_compare_fusion.5
  106.7 1.3 constant_dynamic-slice_fusion.5
  108.0 1.7 fusion.59
  109.8 2.0 select_reduce_fusion.2
  111.9 0.6 dynamic_slice.60
  113.3 0.2 broadcast_compare_fusion.5
  113.5 1.3 constant_dynamic-slice_fusion.5
  114.8 1.7 fusion.59
  116.5 2.0 select_reduce_fusion.2
  118.7 54.3 %all-gather.7.cloned.1.call-done = bf16[2048,1024]{0,1:T(8,128)(2,1)} async-done(((bf16[512,1024]{0,1:T(8,128)(2,1)}), bf16[2048,1024]{0,1:T(8,128)(2,1)}) %all-gather.7.cloned.1.call-update) | async-done | bytes 4194320 | tf_op jit(solution)/shard_map/all_gather | solution.py:43
  173.0 34.2 %while.31 = (s32[]{:T(128)}, f32[512,8,128]{0,2,1:T(8,128)}, s32[4]{0:T(128)S(1)}, bf16[2048,1024]{0,1:T(8,128)(2,1)}, s32[6]{0:T(128)S(1)}, /*index=5*/bf16[204...) while((s32[]{:T(128)}, f32[512,8,128]{0,2,1:T(8,128)}, ...), condition=%wide.region_9.10_spmd.clone, body=%wide.region_6.9_spmd.clone.sunk | while | flops 1083460608 | bytes 12099821 | solution.py:104
  173.0 0.6 dynamic_slice.62
  174.3 0.2 broadcast_compare_fusion.6
  174.6 1.7 constant_dynamic-slice_fusion.6
  176.3 4.0 bitcast_add_fusion.2
  180.3 0.6 dynamic_slice.62
  181.6 0.2 broadcast_compare_fusion.6
  181.9 1.8 constant_dynamic-slice_fusion.6
  183.7 5.7 bitcast_add_fusion.2
  189.3 0.6 dynamic_slice.62
  190.7 0.2 broadcast_compare_fusion.6
  190.9 1.7 constant_dynamic-slice_fusion.6
  192.6 5.6 bitcast_add_fusion.2
  198.2 0.6 dynamic_slice.62
  199.6 0.2 broadcast_compare_fusion.6
  199.8 1.7 constant_dynamic-slice_fusion.6
  201.5 5.6 bitcast_add_fusion.2
  207.2 1.8 convert_element_type.76
  209.0 1.3 copy.73
  210.4 0.1 convert_reduce_fusion.4
  210.6 0.8 broadcast_compare_fusion.2
  211.3 42.5 %all-gather.15.cloned.1.call-done = bf16[2048,1024]{1,0:T(8,128)(2,1)} async-done(((bf16[512,1024]{1,0:T(8,128)(2,1)}), bf16[2048,1024]{1,0:T(8,128)(2,1)}) %all-gather.15.cloned.1.call-update) | async-done | bytes 4194320 | tf_op jit(solution)/shard_map/all_gather | solution.py:108
  253.8 6.4 copy.65
  260.2 11.3 %all_gather.25 = f32[2048,8]{0,1:T(8,128)S(1)} all-gather(f32[512,8]{0,1:T(8,128)S(1)} %bitcast.132), channel_id=1, replica_groups=mesh['heads'=4,'tokens'=4,'cols'=2] {'tokens'}, dimensions={0}, use_global_device_ids=true | all-gather | bytes 81920 | tf_op jit(solution)/shard_map/all_gather | solution.py:106
  271.5 64.1 %all-gather.13.cloned.1.call-done = bf16[2048,1024]{0,1:T(8,128)(2,1)} async-done(((bf16[512,1024]{0,1:T(8,128)(2,1)}), bf16[2048,1024]{0,1:T(8,128)(2,1)}) %all-gather.13.cloned.1.call-update) | async-done | bytes 4194320 | tf_op jit(solution)/shard_map/all_gather | solution.py:107
  335.5 14.4 %fusion.29 = bf16[8,512,128]{1,2,0:T(8,128)(2,1)S(1)} fusion(bf16[2048,8,128]{0,2,1:T(8,128)(2,1)} %bitcast.130, bf16[2048,8,128]{0,2,1:T(8,128)(2,1)} %bitcast.134, f32[8,2048]{1,0:T(8,128)S(1)} %bitcast.133, pred[2048,512]{1,0:T(8,128)(4,1)S(1)} %broadcast_compare_fusion.2, bf16[512,1024]{1,0:T(8,128)(2,1)S(1)} %copy-done.2), kind=kOutput, calls=%fused_computation.50 | convolution fusion | flops 4329046016 | bytes 11599872 | tf_op jit(solution)/shard_map/hqk,qhd->khd/dot_general | solution.py:118
  349.9 1.3 copy.66
  351.3 0.3 all-reduce.3.cloned.1.call-start
  351.6 108.6 %all-gather.11.cloned.1.call-done = bf16[8,512,1024]{2,1,0:T(8,128)(2,1)} async-done(((bf16[1,512,1024]{2,1,0:T(8,128)(2,1)}), bf16[8,512,1024]{2,1,0:T(8,128)(2,1)}) %all-gather.11.cloned.1.call-update) | async-done | bytes 8388624 | tf_op jit(solution)/shard_map/all_gather | solution.py:125
  460.2 4.5 fusion.27
  464.6 120.8 %all-gather.17.cloned.1.call-done = bf16[8,512,1024]{2,1,0:T(8,128)(2,1)} async-done(((bf16[1,512,1024]{2,1,0:T(8,128)(2,1)}), bf16[8,512,1024]{2,1,0:T(8,128)(2,1)}) %all-gather.17.cloned.1.call-update) | async-done | bytes 8388624 | tf_op jit(solution)/shard_map/all_gather | solution.py:126
  585.4 4.4 fusion.26
  589.9 11.5 %copy.60 = bf16[2,1024,4,512]{3,1,0,2:T(8,128)(2,1)} copy(bf16[2,1024,4,512]{1,3,0,2:T(8,128)(2,1)} %bitcast.124) | data formatting | bytes 16777216 | tf_op jit(solution)/shard_map/acnf,ang->cfg/dot_general | solution.py:138
  601.4 11.5 %copy.67 = bf16[2,1024,4,512]{3,1,0,2:T(8,128)(2,1)} copy(bf16[2,1024,4,512]{1,3,0,2:T(8,128)(2,1)} %bitcast.126) | data formatting | bytes 16777216 | tf_op jit(solution)/shard_map/acnf,ang->cfg/dot_general | solution.py:141
  612.9 128.1 %all-reduce.3.cloned.1.call-done = (bf16[4,512,1024]{2,1,0:T(8,128)(2,1)}, bf16[4,512,1024]{2,1,0:T(8,128)(2,1)}) async-done(((bf16[4,512,1024]{2,1,0:T(8,128)(2,1)}, bf16[4,512,1024]{2,1,0:T(8,128)(2,1)}), (bf16[4,512,1024]{2,1,0:T(8,128)(2,1)}, bf16[4,512,1024]{2,1,0:T(8,128)(2,1)})) %all-reduce.3.cloned.1.call-update) | async-done | bytes 8388624 | tf_op jit(solution)/shard_map/psum | solution.py:16
  741.0 14.6 %bitcast_multiply_fusion.1 = f32[2048,1024]{1,0:T(8,128)} fusion(bf16[2048,4,512]{2,0,1:T(8,128)(2,1)} %bitcast.128, bf16[4,512,1024]{2,1,0:T(8,128)(2,1)} %get-tuple-element.383), kind=kOutput, calls=%fused_computation.43 | convolution fusion | flops 8592031744 | bytes 20971520 | tf_op jit(solution)/shard_map/acnf,ang->cfg/dot_general | solution.py:138
  755.6 11.0 %bitcast_multiply_fusion = f32[2048,1024]{1,0:T(8,128)} fusion(bf16[2048,4,512]{2,0,1:T(8,128)(2,1)S(1)} %bitcast.127, bf16[4,512,1024]{2,1,0:T(8,128)(2,1)S(1)} %copy-done.4), kind=kOutput, calls=%fused_computation.42 | convolution fusion | flops 8592031744 | bytes 20971520 | tf_op jit(solution)/shard_map/acnf,ang->cfg/dot_general | solution.py:141
  (76 shorter events, 1.4 us)
Async XLA Ops:
  7.2 84.4 %copy-start = (bf16[512,1024]{1,0:T(8,128)(2,1)S(1)}, bf16[512,1024]{1,0:T(8,128)(2,1)}, u32[]{:S(2)}) copy-start(bf16[512,1024]{1,0:T(8,128)(2,1)} %param.9) | copy-start | bytes 3145732
  7.2 84.4 %copy-start.3 = (s32[6]{0:T(128)S(1)}, s32[6]{0:T(128)}, u32[]{:S(2)}) copy-start(s32[6]{0:T(128)} %param.13) | copy-start | bytes 76
  7.2 84.4 %all-gather.9.cloned.1.call-start = ((), (), s32[]{:S(2)}) async-start(), calls=%async_computation.1 | async-start | bytes 5242880 | tf_op jit(solution)/shard_map/all_gather | solution.py:42
  9.6 163.4 %all-gather.7.cloned.1.call-start = ((), (), s32[]{:S(2)}) async-start(), calls=%async_computation | async-start | bytes 5242880 | tf_op jit(solution)/shard_map/all_gather | solution.py:43
  12.0 241.8 %all-gather.15.cloned.1.call-start = ((), (), s32[]{:S(2)}) async-start(), calls=%async_computation.4 | async-start | bytes 5242880 | tf_op jit(solution)/shard_map/all_gather | solution.py:108
  12.7 322.8 %all-gather.13.cloned.1.call-start = ((), (), s32[]{:S(2)}) async-start(), calls=%async_computation.3 | async-start | bytes 5242880 | tf_op jit(solution)/shard_map/all_gather | solution.py:107
  15.0 445.1 %all-gather.11.cloned.1.call-start = ((), (), s32[]{:S(2)}) async-start(), calls=%async_computation.2 | async-start | bytes 9437184 | tf_op jit(solution)/shard_map/all_gather | solution.py:125
  207.1 128.4 %copy-start.2 = (bf16[512,1024]{1,0:T(8,128)(2,1)S(1)}, bf16[512,1024]{1,0:T(8,128)(2,1)}, u32[]{:S(2)}) copy-start(bf16[512,1024]{1,0:T(8,128)(2,1)} %param.10) | copy-start | bytes 3145732
  210.3 375.1 %all-gather.17.cloned.1.call-start = ((), (), s32[]{:S(2)}) async-start(), calls=%async_computation.5 | async-start | bytes 9437184 | tf_op jit(solution)/shard_map/all_gather | solution.py:126
  351.3 389.7 %all-reduce.3.cloned.1.call-start = ((), (), s32[]{:S(2)}) async-start(), calls=%async_computation.6 | async-start | bytes 16777216 | tf_op jit(solution)/shard_map/psum | solution.py:16
  741.0 14.6 %copy-start.1 = (bf16[2,1024,4,512]{3,1,0,2:T(8,128)(2,1)S(1)}, bf16[2,1024,4,512]{3,1,0,2:T(8,128)(2,1)}, u32[]{:S(2)}) copy-start(bf16[2,1024,4,512]{3,1,0,2:T(8,128)(2,1)} %copy.67) | copy-start | bytes 25165828
  741.0 14.6 %copy-start.4 = (bf16[4,512,1024]{2,1,0:T(8,128)(2,1)S(1)}, bf16[4,512,1024]{2,1,0:T(8,128)(2,1)}, u32[]{:S(2)}) copy-start(bf16[4,512,1024]{2,1,0:T(8,128)(2,1)} %get-tuple-element.384) | copy-start | bytes 12582916
Sparse Core Ops, SparseCore 0:
  9.7 81.7 all-gather.8
  93.7 79.2 all-gather.6
  174.5 79.1 all-gather.14
  255.2 80.2 all-gather.12
  338.1 122.0 all-gather.10
  462.7 122.6 all-gather.16
  590.0 150.9 all-reduce.2
where the time goes:
time: 777 us; the launch traced here: 773 us
  waiting for transfers between devices  596 us (77%)
  matrix products  67.9 us (9%)
  local copies, waits for them, and re-layouts  55.9 us (7%)
  other arithmetic  22.4 us (3%)
  between operations  14.2 us (2%)
  blocking collectives  11.3 us (1%)
    psum x1, waiting for transfers between devices, spread(): return lax.psum(kept, axis)  128 us
    all_gather x1, waiting for transfers between devices, on_device(): lax.all_gather(value_grads[None], ('tokens', 'cols'), axis=0, tiled=True)  121 us
    all_gather x1, waiting for transfers between devices, on_device(): lax.all_gather(attended[None], ('tokens', 'cols'), axis=0, tiled=True)  109 us
    all_gather x1, waiting for transfers between devices, on_device(): lax.all_gather(key_in, 'tokens', axis=0, tiled=True)  76.4 us
    all_gather x1, waiting for transfers between devices, on_device(): query_rows = lax.all_gather(query_in, 'tokens', axis=0, tiled=True)  64.1 us
    all_gather x1, waiting for transfers between devices, on_device(): lax.all_gather(value_in, 'tokens', axis=0, tiled=True)  54.3 us
    all_gather x1, waiting for transfers between devices, on_device(): grad_rows = lax.all_gather(out_grads, 'tokens', axis=0, tiled=True)  42.5 us
    dot_general x4, matrix products, update(): jnp.einsum('hqk,khd->qhd', weights, value_rows, preferred_element_type=jn...  20.9 us
  transfers between devices with their start and end apart: 7, of which 7 were waited for; matrix products, arithmetic and copies ran while one was open for 15% of the time, Pallas kernels for 0%

commit v1 on v0

--- a/solution.py
+++ b/solution.py
@@ -3,6 +3,8 @@
 import jax
 import jax.numpy as jnp
 from jax import lax
+from jax.experimental import pallas as pl
+from jax.experimental.pallas import tpu as pltpu
 from jax.sharding import PartitionSpec as P
 
 HEAD_DIM = 128
@@ -146,6 +148,315 @@
     return (input_factor, grad_factor)
 
 
+BLOCK_Q = 256
+F32 = jnp.float32
+BF16 = jnp.bfloat16
+
+
+def fused_kernel(
+    q_ref, k_ref, v_ref, g_ref, dk_ref, dq_ref, out_a, out_g,
+    xin, rows, cols, v_t, g_acc, stage,
+    own_sem, a2a_send, a2a_recv, row_recv, x_send, up_send, down_send,
+    col_recv, pair_send, y_send, relay_send, out_sem,
+):
+    n = lax.axis_size("tokens")
+    tok_dev = q_ref.shape[0]
+    all_tokens = n * tok_dev
+    h = lax.axis_index("heads")
+    z = lax.axis_index("tokens")
+    x = lax.axis_index("cols")
+    y = h // 2
+    core = h % 2
+    other_x = 1 - x
+    pair = y * 2 + (1 - core)
+    inputs = (q_ref, k_ref, v_ref, g_ref)
+
+    barrier = pltpu.get_barrier_semaphore()
+    for step in range(1, n):
+        pl.semaphore_signal(barrier, inc=1, device_id={"tokens": (z + step) % n})
+    for step in range(1, 4):
+        pl.semaphore_signal(barrier, inc=1, device_id={"heads": (h + step) % 4})
+    pl.semaphore_signal(barrier, inc=1, device_id={"cols": other_x})
+    pl.semaphore_wait(barrier, n + 3)
+
+    def a2a_copy(j, a, step):
+        target = (z + step) % n
+        return pltpu.make_async_remote_copy(
+            src_ref=inputs[a].at[:, pl.ds(pl.multiple_of((j * n + target) * 128, 128), 128)],
+            dst_ref=xin.at[j, a, pl.ds(pl.multiple_of(z * tok_dev, tok_dev), tok_dev), :],
+            send_sem=a2a_send.at[j, a, step],
+            recv_sem=a2a_recv.at[j, a, step],
+            device_id={"tokens": target},
+        )
+
+    def own_copy(j, a):
+        return pltpu.make_async_copy(
+            inputs[a].at[:, pl.ds(pl.multiple_of((j * n + z) * 128, 128), 128)],
+            xin.at[j, a, pl.ds(pl.multiple_of(z * tok_dev, tok_dev), tok_dev), :],
+            own_sem.at[j, a],
+        )
+
+    for j in range(2):
+        for a in range(4):
+            for step in (2, 1, 3):
+                a2a_copy(j, a, step).start()
+            own_copy(j, a).start()
+
+    def attention(j):
+        for a in range(4):
+            own_copy(j, a).wait()
+            for step in range(1, n):
+                a2a_copy(j, a, step).wait()
+        v_t[...] = xin[j, 2].astype(F32).T.astype(BF16)
+        g_acc[...] = jnp.zeros_like(g_acc)
+
+        def block(ib, carry):
+            span = pl.ds(pl.multiple_of(ib * BLOCK_Q, BLOCK_Q), BLOCK_Q)
+            s = lax.dot_general(
+                xin[j, 1], xin[j, 0, span, :], (((1,), (1,)), ((), ())),
+                preferred_element_type=F32,
+            ) * (1.0 / math.sqrt(HEAD_DIM))
+            s = jnp.where(dk_ref[...] == dq_ref[:, span], s, MASK_FLOOR)
+            e = jnp.exp(s - jnp.max(s, axis=0, keepdims=True))
+            p = (e * (1.0 / jnp.sum(e, axis=0, keepdims=True))).astype(BF16)
+            att = jnp.dot(v_t[...], p, preferred_element_type=F32)
+            rows[j, 0, x, z, :, span] = att.astype(BF16)
+            g_acc[...] += jnp.dot(p, xin[j, 3, span, :], preferred_element_type=F32)
+            return carry
+
+        lax.fori_loop(0, all_tokens // BLOCK_Q, block, 0)
+        rows[j, 1, x, z] = g_acc[...].T.astype(BF16)
+
+    def row_copy(j, f, xs, zs, send, device):
+        piece = rows.at[j, f, xs, zs]
+        return pltpu.make_async_remote_copy(
+            src_ref=piece, dst_ref=piece, send_sem=send.at[j, f, zs],
+            recv_sem=row_recv.at[j, f, xs, zs], device_id=device,
+        )
+
+    def x_copy(j, f, zs):
+        return row_copy(j, f, x, zs, x_send, {"cols": other_x})
+
+    def up_copy(j, f, zs):
+        return row_copy(j, f, x, zs, up_send, {"tokens": (z + 1) % n})
+
+    def down_copy(j, f, zs):
+        return row_copy(j, f, x, zs, down_send, {"tokens": (z + n - 1) % n})
+
+    def col_copy(j, f, zs, source, send, device):
+        return pltpu.make_async_remote_copy(
+            src_ref=source, dst_ref=cols.at[j, f, zs], send_sem=send.at[j, f, zs],
+            recv_sem=col_recv.at[j, f, zs], device_id={"heads": device},
+        )
+
+    def pair_copy(j, f, zs):
+        return col_copy(j, f, zs, rows.at[j, f, x, zs], pair_send, pair)
+
+    def y_copy(j, f, zs):
+        return col_copy(j, f, zs, rows.at[j, f, x, zs], y_send, (1 - y) * 2 + zs % 2)
+
+    def relay_copy(j, f, zs):
+        return col_copy(j, f, zs, cols.at[j, f, zs], relay_send, pair)
+
+    is_source = h == z
+    far = y != z // 2
+
+    def feed_cols(j, f, zs):
+        @pl.when(is_source)
+        def _():
+            pair_copy(j, f, zs).start()
+            y_copy(j, f, zs).start()
+
+    def send_own(j, f):
+        @pl.when(z < n - 1)
+        def _():
+            up_copy(j, f, z).start()
+
+        @pl.when(z > 0)
+        def _():
+            down_copy(j, f, z).start()
+
+        x_copy(j, f, z).start()
+        feed_cols(j, f, z)
+
+    def relay_step(j, f, step):
+        @pl.when(z >= step)
+        def _():
+            zs = z - step
+            x_copy(j, f, zs).wait_recv()
+
+            @pl.when(z < n - 1)
+            def _():
+                up_copy(j, f, zs).start()
+
+            x_copy(j, f, zs).start()
+            feed_cols(j, f, zs)
+
+        @pl.when(z + step < n)
+        def _():
+            zs = z + step
+            x_copy(j, f, zs).wait_recv()
+
+            @pl.when(z > 0)
+            def _():
+                down_copy(j, f, zs).start()
+
+            x_copy(j, f, zs).start()
+            feed_cols(j, f, zs)
+
+    def relay_cols(j, f):
+        for zs in range(n):
+            @pl.when(far & (core == zs % 2))
+            def _():
+                relay_copy(j, f, zs).wait_recv()
+                relay_copy(j, f, zs).start()
+
+    def finish(j, f):
+        def one(zs, carry):
+            row_copy(j, f, other_x, zs, x_send, {"cols": other_x}).wait_recv()
+            return carry
+
+        lax.fori_loop(0, n, one, 0)
+        for zs in range(n):
+            @pl.when((h != z) & jnp.logical_not(far & (core == zs % 2)))
+            def _():
+                relay_copy(j, f, zs).wait_recv()
+
+        @pl.when(is_source)
+        def _():
+            def move(zs, carry):
+                cols[j, f, zs] = rows[j, f, x, zs]
+                return carry
+
+            lax.fori_loop(0, n, move, 0)
+
+    used = [0]
+    span_rows = n * 128
+
+    def out_copy(f, xs, jr, jc, slot):
+        target = (out_a, out_g)[f]
+        return pltpu.make_async_copy(
+            stage.at[slot],
+            target.at[
+                pl.ds(pl.multiple_of(xs * (2 * span_rows) + jr * span_rows, span_rows), span_rows),
+                pl.ds(jc * span_rows, span_rows),
+            ],
+            out_sem.at[slot],
+        )
+
+    def tiles(f, xs, jr, jc):
+        slot = used[0] % 2
+        if used[0] >= 2:
+            out_copy(f, xs, jr, jc, slot).wait()
+        used[0] += 1
+
+        def part(m, carry):
+            left = rows[jr, f, xs, pl.ds(2 * m, 2)].reshape(256, all_tokens)
+            right = cols[jc, f].reshape(span_rows, all_tokens)
+            stage[slot, pl.ds(pl.multiple_of(m * 256, 256), 256), :] = lax.dot_general(
+                left, right, (((1,), (1,)), ((), ())), preferred_element_type=F32
+            ) * (1.0 / all_tokens)
+            return carry
+
+        lax.fori_loop(0, n // 2, part, 0)
+        out_copy(f, xs, jr, jc, slot).start()
+
+    attention(0)
+    send_own(0, 0)
+    send_own(0, 1)
+    attention(1)
+    send_own(1, 0)
+    send_own(1, 1)
+    for f in range(2):
+        for step in range(1, n):
+            relay_step(0, f, step)
+        relay_cols(0, f)
+    for step in range(1, n):
+        relay_step(1, 0, step)
+    relay_cols(1, 0)
+    early = []
+    for f in range(2):
+        early += [(f, x, 0, 0), (f, other_x, 0, 0)]
+    finish(0, 0)
+    finish(0, 1)
+    for step in range(1, n):
+        relay_step(1, 1, step)
+        if step < n:
+            tiles(*early[step - 1])
+    relay_cols(1, 1)
+    for item in early[n - 1:]:
+        tiles(*item)
+    for f in range(2):
+        finish(1, f)
+        for xs in (x, other_x):
+            for jr, jc in ((0, 1), (1, 0), (1, 1)):
+                tiles(f, xs, jr, jc)
+    for slot in range(2):
+        out_copy(0, x, 0, 0, slot).wait()
+
+    for j in range(2):
+        for f in range(2):
+            for zs in range(n):
+                x_copy(j, f, zs).wait_send()
+
+                @pl.when((z < n - 1) & (zs <= z))
+                def _():
+                    up_copy(j, f, zs).wait_send()
+
+                @pl.when((z > 0) & (zs >= z))
+                def _():
+                    down_copy(j, f, zs).wait_send()
+
+                @pl.when(is_source)
+                def _():
+                    pair_copy(j, f, zs).wait_send()
+                    y_copy(j, f, zs).wait_send()
+
+                @pl.when(far & (core == zs % 2))
+                def _():
+                    relay_copy(j, f, zs).wait_send()
+
+
+def fused(query_in, key_in, value_in, out_grads, doc_starts):
+    n = lax.axis_size("tokens")
+    tok_dev, row_width = query_in.shape
+    all_tokens = n * tok_dev
+    docs = document_ids(jnp.arange(all_tokens, dtype=jnp.int32), doc_starts)
+    dma = pltpu.SemaphoreType.DMA
+    hbm = pl.BlockSpec(memory_space=pl.ANY)
+    vmem = pl.BlockSpec(memory_space=pltpu.VMEM)
+    out = jax.ShapeDtypeStruct((2 * row_width, row_width), F32)
+    return tuple(pl.pallas_call(
+        fused_kernel,
+        out_shape=(out, out),
+        in_specs=[hbm] * 4 + [vmem] * 2,
+        out_specs=[hbm] * 2,
+        scratch_shapes=[
+            pltpu.VMEM((2, 4, all_tokens, HEAD_DIM), BF16),
+            pltpu.VMEM((2, 2, 2, n, HEAD_DIM, all_tokens), BF16),
+            pltpu.VMEM((2, 2, n, HEAD_DIM, all_tokens), BF16),
+            pltpu.VMEM((HEAD_DIM, all_tokens), BF16),
+            pltpu.VMEM((all_tokens, HEAD_DIM), F32),
+            pltpu.VMEM((2, n * HEAD_DIM, n * HEAD_DIM), F32),
+            dma((2, 4)), dma((2, 4, n)), dma((2, 4, n)),
+            dma((2, 2, 2, n)), dma((2, 2, n)), dma((2, 2, n)), dma((2, 2, n)),
+            dma((2, 2, n)), dma((2, 2, n)), dma((2, 2, n)), dma((2, 2, n)),
+            dma((2,)),
+        ],
+        compiler_params=pltpu.CompilerParams(
+            collective_id=0, has_side_effects=True, vmem_limit_bytes=60 * 1024 * 1024
+        ),
+    )(query_in, key_in, value_in, out_grads, docs[:, None], docs[None, :]))
+
+
+def per_device(query_in, key_in, value_in, out_grads, doc_starts):
+    n = lax.axis_size("tokens")
+    fits = n == 4 and lax.axis_size("heads") == 4 and lax.axis_size("cols") == 2
+    if fits and query_in.shape[1] == 2 * n * HEAD_DIM and query_in.shape[0] % BLOCK_Q == 0:
+        return fused(query_in, key_in, value_in, out_grads, doc_starts)
+    return on_device(query_in, key_in, value_in, out_grads, doc_starts)
+
+
 def solution(mesh):
     in_specs = (
         P("tokens", ("heads", "cols")),
@@ -156,5 +467,5 @@
     )
     out_specs = (P("heads", ("tokens", "cols")), P("heads", ("tokens", "cols")))
     return jax.shard_map(
-        on_device, mesh=mesh, in_specs=in_specs, out_specs=out_specs, check_vma=False
-    )
+        per_device, mesh=mesh, in_specs=in_specs, out_specs=out_specs, check_vma=False
+    )

time: 777 us -> 307 us (0.40)
  waiting for transfers between devices: 596 us -> 0 us
  Pallas kernels: 0 us -> 290 us
  matrix products: 67.9 us -> 0 us
  local copies, waits for them, and re-layouts: 55.9 us -> 13.3 us
  other arithmetic: 22.4 us -> 0.75 us
  between operations: 14.2 us -> 0.67 us
  blocking collectives: 11.3 us -> 0 us
    all_gather x6 -> x0, waiting for transfers between devices: 467 us -> none  [the longest x1 121 us: on_device(): lax.all_gather(value_grads[None], ('tokens', 'cols'), axis=0, tiled=True)]
    pallas_call x0 -> x1, Pallas kernels: none -> 290 us  [fused(): pl.pallas_call(fused_kernel, out_shape=(out, out), in_specs=[hbm] * 4 + [...]
    psum x1 -> x0, waiting for transfers between devices: 128 us -> none  [spread(): return lax.psum(kept, axis)]
    dot_general x11 -> x0, matrix products: 67.9 us -> none  [the longest x4 20.9 us: update(): jnp.einsum('hqk,khd->qhd', weights, value_rows, preferred_element_type=jn...]
    dot_general x2 -> x0, local copies, waits for them, and re-layouts: 23 us -> none  [the longest x1 11.5 us: on_device(): jnp.einsum('acnf,ang->cfg', rows_grads, cols_grads, preferred_element_typ...]
    dynamic_slice x16 -> x0, local copies, waits for them, and re-layouts: 16.9 us -> none  [the longest x8 12.2 us: block_scores(): key_rows = lax.dynamic_slice_in_dim(keys_all, key_begin, key_span, 0)]
    all_gather x1 -> x0, blocking collectives: 11.3 us -> none  [on_device(): stats_all = lax.all_gather(log_total.T, 'tokens', axis=0, tiled=True)]
    select_n x2 -> x0, other arithmetic: 8.91 us -> none  [spread(): jnp.where(lax.axis_index(axis) == source, value, 0).astype(value.dtype)]
  transfers between devices with their start and end apart: 7 -> 0, of which waited for: 7 -> 0; matrix products, arithmetic and copies ran while one was open for 15% -> 0% of each run, Pallas kernels for 0% -> 0%
where the time goes in v1:
time: 307 us; the launch traced here: 304 us
  Pallas kernels  290 us (94%)
  local copies, waits for them, and re-layouts  13.3 us (4%)
    pallas_call x1, Pallas kernels, fused(): pl.pallas_call(fused_kernel, out_shape=(out, out), in_specs=[hbm] * 4 + [...  290 us
    unnamed x6, local copies, waits for them, and re-layouts  12 us

profile of v1, /device:TPU:5, one launch (start us, length us, event | category | flops | bytes accessed | tf_op | source)
XLA Modules:
  0.0 304.3 jit_solution(11182892967911254959)
XLA Ops:
  0.6 0.7 convert_reduce_fusion
  1.4 0.0 copy-start.1
  1.4 1.3 copy.8.dk_ref
  2.8 0.0 copy-done.1
  2.8 289.5 %shard_map.68 = (f32[2048,1024]{1,0:T(8,128)}, f32[2048,1024]{1,0:T(8,128)}) custom-call(bf16[512,1024]{1,0:T(8,128)(2,1)} %q_ref.1, bf16[512,1024]{1,0:T(8,128)(2,1)} %k_ref.1, bf16[512,1024]{1,0:T(8,128)(2,1)} %v_ref.1, bf16[512,1024]{1,0:T(8,128)(2,1)} %g_ref.1, s32[2048,1]{1,0:T(8,128)} %copy.8.dk_ref, s32[1,2048]{1,0:T(1,128)} %bitcast.3), custom_call_target="tpu_custom_call" | custom-call | tf_op jit(solution)/shard_map/pallas_call | solution.py:429
  292.3 0.0 copy-start
  292.3 8.6 %copy.11 = f32[2048,1024]{1,0:T(8,128)} copy(f32[2048,1024]{1,0:T(8,128)} %get-tuple-element.4) | data formatting | bytes 16777216
  300.9 0.0 copy-done
  300.9 3.4 %copy.12 = f32[2048,1024]{1,0:T(8,128)} copy(f32[2048,1024]{1,0:T(8,128)S(1)} %copy-done) | data formatting | bytes 16777216
  (1 shorter events, 0.0 us)
Async XLA Ops:
  1.4 1.4 copy-start.1
  292.3 8.6 %copy-start = (f32[2048,1024]{1,0:T(8,128)S(1)}, f32[2048,1024]{1,0:T(8,128)}, u32[]{:S(2)}) copy-start(f32[2048,1024]{1,0:T(8,128)} %get-tuple-element.5) | copy-start | bytes 25165828

commit v2 on v1

--- a/solution.py
+++ b/solution.py
@@ -149,6 +149,7 @@
 
 
 BLOCK_Q = 256
+SWAPPED = ((0, 1), (1, 0))
 F32 = jnp.float32
 BF16 = jnp.bfloat16
 
@@ -157,7 +158,7 @@
     q_ref, k_ref, v_ref, g_ref, dk_ref, dq_ref, out_a, out_g,
     xin, rows, cols, v_t, g_acc, stage,
     own_sem, a2a_send, a2a_recv, row_recv, x_send, up_send, down_send,
-    col_recv, pair_send, y_send, relay_send, out_sem,
+    col_recv, pair_send, y_send, relay_send, swap_send, out_sem,
 ):
     n = lax.axis_size("tokens")
     tok_dev = q_ref.shape[0]
@@ -196,7 +197,7 @@
             own_sem.at[j, a],
         )
 
-    for j in range(2):
+    def send_inputs(j):
         for a in range(4):
             for step in (2, 1, 3):
                 a2a_copy(j, a, step).start()
@@ -207,6 +208,8 @@
             own_copy(j, a).wait()
             for step in range(1, n):
                 a2a_copy(j, a, step).wait()
+        if j == 0:
+            send_inputs(1)
         v_t[...] = xin[j, 2].astype(F32).T.astype(BF16)
         g_acc[...] = jnp.zeros_like(g_acc)
 
@@ -258,6 +261,24 @@
     def relay_copy(j, f, zs):
         return col_copy(j, f, zs, cols.at[j, f, zs], relay_send, pair)
 
+    mate = z + 1 - 2 * (z % 2)
+
+    def swap_copy(j, f, zs):
+        return row_copy(j, f, other_x, zs, swap_send, {"tokens": mate})
+
+    def swap(j, f):
+        x_copy_in = row_copy(j, f, other_x, z, x_send, {"cols": other_x})
+        x_copy_in.wait_recv()
+        swap_copy(j, f, z).start()
+
+    def relay_x(j, f, zs):
+        if (j, f) in SWAPPED:
+            @pl.when(zs != mate)
+            def _():
+                x_copy(j, f, zs).start()
+        else:
+            x_copy(j, f, zs).start()
+
     is_source = h == z
     far = y != z // 2
 
@@ -289,7 +310,7 @@
             def _():
                 up_copy(j, f, zs).start()
 
-            x_copy(j, f, zs).start()
+            relay_x(j, f, zs)
             feed_cols(j, f, zs)
 
         @pl.when(z + step < n)
@@ -301,7 +322,7 @@
             def _():
                 down_copy(j, f, zs).start()
 
-            x_copy(j, f, zs).start()
+            relay_x(j, f, zs)
             feed_cols(j, f, zs)
 
     def relay_cols(j, f):
@@ -311,12 +332,20 @@
                 relay_copy(j, f, zs).wait_recv()
                 relay_copy(j, f, zs).start()
 
-    def finish(j, f):
+    def finish_rows(j, f):
         def one(zs, carry):
-            row_copy(j, f, other_x, zs, x_send, {"cols": other_x}).wait_recv()
+            waiting = row_copy(j, f, other_x, zs, x_send, {"cols": other_x})
+            if (j, f) in SWAPPED:
+                @pl.when(zs != z)
+                def _():
+                    waiting.wait_recv()
+            else:
+                waiting.wait_recv()
             return carry
 
         lax.fori_loop(0, n, one, 0)
+
+    def finish_cols(j, f):
         for zs in range(n):
             @pl.when((h != z) & jnp.logical_not(far & (core == zs % 2)))
             def _():
@@ -361,43 +390,63 @@
         lax.fori_loop(0, n // 2, part, 0)
         out_copy(f, xs, jr, jc, slot).start()
 
+    send_inputs(0)
     attention(0)
     send_own(0, 0)
     send_own(0, 1)
+
+    def relay(j, f, step):
+        relay_step(j, f, step)
+        if step == 1 and (j, f) in SWAPPED:
+            swap(j, f)
+
+    relay(0, 0, 1)
+    relay(0, 1, 1)
     attention(1)
     send_own(1, 0)
     send_own(1, 1)
     for f in range(2):
-        for step in range(1, n):
-            relay_step(0, f, step)
+        for step in range(2, n):
+            relay(0, f, step)
         relay_cols(0, f)
     for step in range(1, n):
-        relay_step(1, 0, step)
+        relay(1, 0, step)
     relay_cols(1, 0)
     early = []
     for f in range(2):
+        finish_rows(0, f)
+        finish_cols(0, f)
         early += [(f, x, 0, 0), (f, other_x, 0, 0)]
-    finish(0, 0)
-    finish(0, 1)
     for step in range(1, n):
-        relay_step(1, 1, step)
-        if step < n:
-            tiles(*early[step - 1])
+        relay(1, 1, step)
+        tiles(*early[step - 1])
     relay_cols(1, 1)
     for item in early[n - 1:]:
         tiles(*item)
     for f in range(2):
-        finish(1, f)
-        for xs in (x, other_x):
-            for jr, jc in ((0, 1), (1, 0), (1, 1)):
-                tiles(f, xs, jr, jc)
+        finish_cols(1, f)
+        for jr, jc in ((0, 1), (1, 0), (1, 1)):
+            tiles(f, x, jr, jc)
+        tiles(f, other_x, 0, 1)
+        finish_rows(1, f)
+        for jc in range(2):
+            tiles(f, other_x, 1, jc)
     for slot in range(2):
         out_copy(0, x, 0, 0, slot).wait()
 
     for j in range(2):
         for f in range(2):
             for zs in range(n):
-                x_copy(j, f, zs).wait_send()
+                if (j, f) in SWAPPED:
+                    @pl.when(zs != mate)
+                    def _():
+                        x_copy(j, f, zs).wait_send()
+
+                    @pl.when(zs == z)
+                    def _():
+                        swap_copy(j, f, zs).wait_send()
+                else:
+                    x_copy(j, f, zs).wait_send()
 
                 @pl.when((z < n - 1) & (zs <= z))
                 def _():
@@ -441,7 +490,7 @@
             dma((2, 4)), dma((2, 4, n)), dma((2, 4, n)),
             dma((2, 2, 2, n)), dma((2, 2, n)), dma((2, 2, n)), dma((2, 2, n)),
             dma((2, 2, n)), dma((2, 2, n)), dma((2, 2, n)), dma((2, 2, n)),
-            dma((2,)),
+            dma((2, 2, n)), dma((2,)),
         ],
         compiler_params=pltpu.CompilerParams(
             collective_id=0, has_side_effects=True, vmem_limit_bytes=60 * 1024 * 1024

time: 307 us -> 291 us (0.948)
  Pallas kernels: 290 us -> 276 us
    pallas_call x1, Pallas kernels: 290 us -> 276 us  [fused(): pl.pallas_call(fused_kernel, out_shape=(out, out), in_specs=[hbm] * 4 + [...]
where the time goes in v2:
time: 291 us
  Pallas kernels  276 us (95%)
  local copies, waits for them, and re-layouts  13.3 us (5%)
    pallas_call x1, Pallas kernels, fused(): pl.pallas_call(fused_kernel, out_shape=(out, out), in_specs=[hbm] * 4 + [...  276 us
    unnamed x6, local copies, waits for them, and re-layouts  12 us

profile of v2, /device:TPU:5, one launch (start us, length us, event | category | flops | bytes accessed | tf_op | source)
XLA Modules:
  0.0 290.6 jit_solution(14338880786466364013)
XLA Ops:
  0.6 0.7 convert_reduce_fusion
  1.4 0.0 copy-start.1
  1.4 1.3 copy.8.dk_ref
  2.8 0.0 copy-done.1
  2.8 275.8 %shard_map.68 = (f32[2048,1024]{1,0:T(8,128)}, f32[2048,1024]{1,0:T(8,128)}) custom-call(bf16[512,1024]{1,0:T(8,128)(2,1)} %q_ref.1, bf16[512,1024]{1,0:T(8,128)(2,1)} %k_ref.1, bf16[512,1024]{1,0:T(8,128)(2,1)} %v_ref.1, bf16[512,1024]{1,0:T(8,128)(2,1)} %g_ref.1, s32[2048,1]{1,0:T(8,128)} %copy.8.dk_ref, s32[1,2048]{1,0:T(1,128)} %bitcast.3), custom_call_target="tpu_custom_call" | custom-call | tf_op jit(solution)/shard_map/pallas_call | solution.py:478
  278.6 0.0 copy-start
  278.6 8.6 %copy.11 = f32[2048,1024]{1,0:T(8,128)} copy(f32[2048,1024]{1,0:T(8,128)} %get-tuple-element.4) | data formatting | bytes 16777216
  287.2 0.0 copy-done
  287.2 3.4 %copy.12 = f32[2048,1024]{1,0:T(8,128)} copy(f32[2048,1024]{1,0:T(8,128)S(1)} %copy-done) | data formatting | bytes 16777216
  (1 shorter events, 0.0 us)
Async XLA Ops:
  1.4 1.4 copy-start.1
  278.6 8.6 %copy-start = (f32[2048,1024]{1,0:T(8,128)S(1)}, f32[2048,1024]{1,0:T(8,128)}, u32[]{:S(2)}) copy-start(f32[2048,1024]{1,0:T(8,128)} %get-tuple-element.5) | copy-start | bytes 25165828

commit v3 on v2

--- a/solution.py
+++ b/solution.py
@@ -405,23 +405,24 @@
     attention(1)
     send_own(1, 0)
     send_own(1, 1)
-    for f in range(2):
-        for step in range(2, n):
-            relay(0, f, step)
-        relay_cols(0, f)
-    for step in range(1, n):
-        relay(1, 0, step)
-    relay_cols(1, 0)
+    for step in range(2, n):
+        relay(0, 0, step)
+        relay(0, 1, step)
+        relay(1, 0, step - 1)
+        relay(1, 1, step - 1)
+    relay_cols(0, 0)
+    relay_cols(0, 1)
     early = []
     for f in range(2):
         finish_rows(0, f)
         finish_cols(0, f)
         early += [(f, x, 0, 0), (f, other_x, 0, 0)]
-    for step in range(1, n):
-        relay(1, 1, step)
-        tiles(*early[step - 1])
+    for f in range(2):
+        tiles(*early[f])
+        relay(1, f, n - 1)
+    relay_cols(1, 0)
     relay_cols(1, 1)
-    for item in early[n - 1:]:
+    for item in early[2:]:
         tiles(*item)
     for f in range(2):
         finish_cols(1, f)

time: 291 us -> 292 us (level)
  no operation moved by 1% of the time
where the time goes in v3:
time: 292 us
  Pallas kernels  277 us (95%)
  local copies, waits for them, and re-layouts  13.3 us (5%)
    pallas_call x1, Pallas kernels, fused(): pl.pallas_call(fused_kernel, out_shape=(out, out), in_specs=[hbm] * 4 + [...  277 us
    unnamed x6, local copies, waits for them, and re-layouts  12 us

profile of v3, /device:TPU:5, one launch (start us, length us, event | category | flops | bytes accessed | tf_op | source)
XLA Modules:
  0.0 292.1 jit_solution(1831983206916090661)
XLA Ops:
  0.6 0.7 convert_reduce_fusion
  1.4 0.0 copy-start.1
  1.4 1.3 copy.8.dk_ref
  2.8 0.0 copy-done.1
  2.8 277.3 %shard_map.68 = (f32[2048,1024]{1,0:T(8,128)}, f32[2048,1024]{1,0:T(8,128)}) custom-call(bf16[512,1024]{1,0:T(8,128)(2,1)} %q_ref.1, bf16[512,1024]{1,0:T(8,128)(2,1)} %k_ref.1, bf16[512,1024]{1,0:T(8,128)(2,1)} %v_ref.1, bf16[512,1024]{1,0:T(8,128)(2,1)} %g_ref.1, s32[2048,1]{1,0:T(8,128)} %copy.8.dk_ref, s32[1,2048]{1,0:T(1,128)} %bitcast.3), custom_call_target="tpu_custom_call" | custom-call | tf_op jit(solution)/shard_map/pallas_call | solution.py:479
  280.1 0.0 copy-start
  280.1 8.6 %copy.11 = f32[2048,1024]{1,0:T(8,128)} copy(f32[2048,1024]{1,0:T(8,128)} %get-tuple-element.4) | data formatting | bytes 16777216
  288.7 0.0 copy-done
  288.7 3.4 %copy.12 = f32[2048,1024]{1,0:T(8,128)} copy(f32[2048,1024]{1,0:T(8,128)S(1)} %copy-done) | data formatting | bytes 16777216
  (1 shorter events, 0.0 us)
Async XLA Ops:
  1.4 1.4 copy-start.1
  280.1 8.6 %copy-start = (f32[2048,1024]{1,0:T(8,128)S(1)}, f32[2048,1024]{1,0:T(8,128)}, u32[]{:S(2)}) copy-start(f32[2048,1024]{1,0:T(8,128)} %get-tuple-element.5) | copy-start | bytes 25165828
